TPU v7x, 32 devices: a whole 2x2x4 slice. The times are simulated.
32 devices in a mesh: mem: 4 (over z), state: 8 (over y, x, core).
Axes of the slice: x: 2, y: 2, z: 4, core: 2. Of those that a mesh axis runs over, the one named last changes fastest.
Arguments:
- anomalies: bfloat16 [64, 32, 32768], P('mem', None, 'state'), may hold values from -0.75 to 0.75
- alpha: bfloat16 [64, 32, 2048], P('mem', None, 'state'), may hold values from -6 to 6
- basis: bfloat16 [2048, 32768], P(None, 'state'), may hold values from -0.1875 to 0.1875
- gradient: bfloat16 [32, 32768], P(None, 'state'), may hold values from -6 to 6
- vertical_root: float32 [32, 32], replicated, may hold values from -1 to 1
- band_gain: float32 [16], replicated, may hold values from 0.25 to 2
- band: int32 [2048], P('state'), may hold values from 0 to 15
- order: int32 [64], replicated, may hold values from 0 to 63, each once
Outputs:
- increment: float32 [32, 32768], P(None, 'state')
- alpha_grad: float32 [64, 32, 2048], P('mem', None, 'state')
Inputs may be any that keep to these rules, and one draw needn't show every extreme that they name: `order`: a permutation: every member is named by exactly one slot.
All inputs are finite; a program needn't handle non-finite values.
Results may differ from a plain program's by a relative error of at most 0.0029.
Values may be sent and summed in bfloat16 or wider, within the bound.
A program may use at most 128 MiB of HBM per device.

v0:
```python
import jax
import jax.numpy as jnp
from jax import lax
from jax.sharding import PartitionSpec as P


def on_device(anomalies, alpha, basis, gradient, vertical_root, band_gain, band, order):
    high = lax.Precision.HIGHEST
    mem_count = lax.axis_size("mem")
    mem_rank = lax.axis_index("mem")
    member_dev, levels, columns = anomalies.shape
    mode_rows = alpha.shape[2]
    bands = band_gain.shape[0]
    onehot = (band[:, None] == jnp.arange(bands, dtype=jnp.int32)[None, :]).astype(jnp.float32)
    filter_gain = jnp.sum(onehot * band_gain[None, :], axis=1)
    coef = jnp.einsum("ab,jbk->jak", vertical_root, alpha.astype(jnp.float32), precision=high)
    coef = (coef * filter_gain[None, None, :]).astype(jnp.bfloat16)
    members = mem_rank * member_dev + jnp.arange(member_dev, dtype=jnp.int32)
    select = (order[None, :] == members[:, None]).astype(jnp.bfloat16)
    state_count = lax.axis_size("state")
    gathered = lax.all_gather(coef[None], ("mem", "state"), axis=0, tiled=True)
    blocks = gathered.reshape(mem_count, state_count, member_dev, levels, mode_rows)
    picked = jnp.einsum(
        "imj,msjlc->ilsc",
        select.reshape(member_dev, mem_count, member_dev),
        blocks,
        preferred_element_type=jnp.float32,
    )
    picked = picked.astype(jnp.bfloat16).reshape(member_dev * levels, state_count * mode_rows)
    member_field = jnp.dot(picked, basis, preferred_element_type=jnp.float32)
    partial_value = jnp.sum(
        anomalies.astype(jnp.float32) * member_field.reshape(member_dev, levels, columns), axis=0
    )
    increment = lax.psum(partial_value, "mem")
    weighted = (anomalies.astype(jnp.float32) * gradient.astype(jnp.float32)[None]).astype(
        jnp.bfloat16
    )
    weighted = weighted.reshape(member_dev * levels, columns)
    projected = lax.psum_scatter(
        lax.dot_general(
            basis, weighted, (((1,), (1,)), ((), ())), preferred_element_type=jnp.float32
        ),
        "state",
        scatter_dimension=0,
        tiled=True,
    )
    member_grad = jnp.einsum(
        "ab,kma->mbk",
        vertical_root,
        projected.reshape(mode_rows, member_dev, levels),
        precision=high,
    )
    member_grad = member_grad * filter_gain[None, None, :]
    placed = jnp.einsum("ij,ibk->jbk", select.astype(jnp.float32), member_grad, precision=high)
    outgoing = placed.reshape(mem_count, member_dev, levels, mode_rows)
    incoming = lax.all_to_all(outgoing, "mem", split_axis=0, concat_axis=0, tiled=True)
    alpha_grad = jnp.sum(incoming, axis=0)
    return (increment, alpha_grad)


def solution(mesh):
    return jax.shard_map(
        on_device,
        mesh=mesh,
        in_specs=(
            P("mem", None, "state"),
            P("mem", None, "state"),
            P(None, "state"),
            P(None, "state"),
            P(),
            P(),
            P("state"),
            P(),
        ),
        out_specs=(P(None, "state"), P("mem", None, "state")),
        check_vma=False,
    )
```

profile of v0, /device:TPU:0, one launch (start us, length us, event | category | flops | bytes accessed | tf_op | source)
XLA Modules:
  0.0 206.5 jit_solution(10233362292895392196)
XLA Ops:
  8.0 0.0 copy-start
  8.0 0.0 reduce-scatter.2.cloned.1.call-start
  8.1 1.0 convert_element_type.31
  9.1 3.3 %fusion.3 = bf16[16,32,4096]{2,1,0:T(8,128)(2,1)S(1)} fusion(bf16[16,32,4096]{2,1,0:T(8,128)(2,1)} %param.8, f32[32,4096]{1,0:T(8,128)S(1)} %convert_element_type.31), kind=kLoop, calls=%fused_computation.5 | loop fusion | flops 6291456 | bytes 8912896 | tf_op jit(solution)/shard_map/convert_element_type | solution.py:35
  12.4 13.7 %convolution_bitcast_fusion = f32[2048,512]{0,1:T(8,128)} fusion(bf16[512,4096]{1,0:T(8,128)(2,1)S(1)} %bitcast.44, bf16[2048,4096]{1,0:T(8,128)(2,1)} %param.10), kind=kOutput, calls=%fused_computation.9 | convolution fusion | flops 8589934592 | bytes 25165824 | tf_op jit(solution)/shard_map/dot_general | solution.py:40
  26.2 0.0 reduce-scatter.2.cloned.1.call-update
  26.2 0.0 all-gather.3.cloned.1.call-start
  26.2 0.6 copy-done.3
  26.8 0.0 copy-done.4
  26.8 0.1 select_reduce_fusion
  26.9 0.0 copy-done
  26.9 0.0 copy-done.1
  26.9 1.1 fusion.15
  28.0 0.0 all-gather.3.cloned.1.call-update
  28.0 0.1 eq.38
  28.1 52.4 %reduce-scatter.2.cloned.1.call-done = f32[256,512]{0,1:T(8,128)} async-done(((f32[2048,512]{0,1:T(8,128)}), f32[256,512]{0,1:T(8,128)}) %reduce-scatter.2.cloned.1.call-update) | async-done | bytes 524304 | tf_op jit(solution)/shard_map/reduce_scatter | solution.py:39
  80.5 1.7 fusion.13
  82.2 1.2 fusion.16
  83.3 1.6 copy.30
  84.9 4.6 %all-to-all-start = ((f32[4,16,32,256]{3,1,2,0:T(8,128)}), f32[4,16,32,256]{3,1,2,0:T(8,128)S(1)}, u32[]{:S(2)}, u32[]{:S(2)}) async-start(f32[4,16,32,256]{3,1,2,0:T(8,128)} %copy.30), calls=%async_computation.1 | async-start | bytes 4194304 | tf_op jit(solution)/shard_map/all_to_all | solution.py:56
  89.5 0.0 all-reduce.2.cloned.1.call-start
  89.5 41.0 %all-gather.3.cloned.1.call-done = bf16[512,32,256]{2,1,0:T(8,128)(2,1)} async-done(((bf16[16,32,256]{2,1,0:T(8,128)(2,1)}), bf16[512,32,256]{2,1,0:T(8,128)(2,1)}) %all-gather.3.cloned.1.call-update) | async-done | bytes 8388624 | tf_op jit(solution)/shard_map/all_gather | solution.py:21
  130.5 8.1 %fusion.10 = bf16[16,32,8,256]{3,0,1,2:T(8,128)(2,1)S(1)} fusion(bf16[4,8,16,32,256]{4,3,2,1,0:T(8,128)(2,1)} %bitcast.46, s32[4,16]{1,0:T(4,128)S(1)} %eq.38, s32[16]{0:T(128)S(1)} %iota_add_fusion), kind=kOutput, calls=%fused_computation.10 | convolution fusion | flops 135267328 | bytes 10486080 | tf_op jit(solution)/shard_map/imj,msjlc->ilsc/dot_general | solution.py:23
  138.6 2.5 %copy.27 = bf16[16,32,8,256]{3,2,1,0:T(8,128)(2,1)} copy(bf16[16,32,8,256]{3,0,1,2:T(8,128)(2,1)S(1)} %fusion.10) | data formatting | bytes 4194304 | tf_op jit(solution)/shard_map/convert_element_type | solution.py:29
  141.1 4.2 %dot_general.24 = bf16[16,32,2048]{2,1,0:T(8,128)(2,1)} reshape(bf16[16,32,8,256]{3,2,1,0:T(8,128)(2,1)} %copy.27) | data formatting | bytes 4194304 | tf_op jit(solution)/shard_map/dot_general | solution.py:30
  145.3 14.4 %fusion.2 = f32[32,4096]{1,0:T(8,128)} fusion(bf16[16,32,4096]{2,1,0:T(8,128)(2,1)} %param.8, bf16[16,32,2048]{2,1,0:T(8,128)(2,1)} %dot_general.24, bf16[2048,4096]{1,0:T(8,128)(2,1)} %param.10), kind=kOutput, calls=%fused_computation.4 | convolution fusion | flops 8596094976 | bytes 23592960 | tf_op jit(solution)/shard_map/dot_general | solution.py:30
  159.8 0.0 all-reduce.2.cloned.1.call-update
  159.8 0.0 all-to-all-done
  159.8 0.2 reduce_sum.29
  160.1 1.1 copy.32
  161.2 36.1 %all-reduce.2.cloned.1.call-done = f32[32,4096]{1,0:T(8,128)} async-done(((f32[32,4096]{1,0:T(8,128)}), f32[32,4096]{1,0:T(8,128)}) %all-reduce.2.cloned.1.call-update) | async-done | bytes 524304 | tf_op jit(solution)/shard_map/psum | solution.py:34
  197.2 1.9 copy.47
  (6 shorter events, 0.0 us)
Async XLA Ops:
  8.0 18.9 %copy-start = (bf16[16,32,256]{2,1,0:T(8,128)(2,1)S(1)}, bf16[16,32,256]{2,1,0:T(8,128)(2,1)}, u32[]{:S(2)}) copy-start(bf16[16,32,256]{2,1,0:T(8,128)(2,1)} %param.9) | copy-start | bytes 786436
  8.0 72.5 %reduce-scatter.2.cloned.1.call-start = ((), (), s32[]{:S(2)}) async-start(), calls=%async_computation.3 | async-start | bytes 4718592 | tf_op jit(solution)/shard_map/reduce_scatter | solution.py:39
  26.2 0.7 copy-start.3
  26.2 0.7 copy-start.4
  26.2 0.8 copy-start.1
  26.2 1.9 copy-start.2
  26.2 104.3 %all-gather.3.cloned.1.call-start = ((), (), s32[]{:S(2)}) async-start(), calls=%async_computation.4 | async-start | bytes 8650752 | tf_op jit(solution)/shard_map/all_gather | solution.py:21
  84.9 74.9 %all-to-all-start = ((f32[4,16,32,256]{3,1,2,0:T(8,128)}), f32[4,16,32,256]{3,1,2,0:T(8,128)S(1)}, u32[]{:S(2)}, u32[]{:S(2)}) async-start(f32[4,16,32,256]{3,1,2,0:T(8,128)} %copy.30), calls=%async_computation.1 | async-start | bytes 4194304 | tf_op jit(solution)/shard_map/all_to_all | solution.py:56
  89.5 107.7 %all-reduce.2.cloned.1.call-start = ((), (), s32[]{:S(2)}) async-start(), calls=%async_computation.2 | async-start | bytes 1048576 | tf_op jit(solution)/shard_map/psum | solution.py:34
Sparse Core Ops, SparseCore 0:
  26.3 54.1 reduce-scatter.1
Sparse Core Ops, SparseCore 1:
  30.1 100.3 all-gather.2
  159.9 37.3 all-reduce.1
where the time goes:
time: 207 us
  waiting for transfers between devices  129 us (62%)
  matrix products  40.2 us (19%)
  between operations  15.6 us (8%)
  local copies, waits for them, and re-layouts  11.9 us (6%)
  starting transfers between devices  4.71 us (2%)
  other arithmetic  4.69 us (2%)
    reduce_scatter x1, waiting for transfers between devices, on_device(): lax.psum_scatter(lax.dot_general(basis, weighted, (((1,), (1,)), ((), ())...  52.4 us
    all_gather x1, waiting for transfers between devices, on_device(): gathered = lax.all_gather(coef[None], ('mem', 'state'), axis=0, tiled=True)  41 us
    psum x1, waiting for transfers between devices, on_device(): increment = lax.psum(partial_value, 'mem')  36.1 us
    dot_general x1, matrix products, on_device(): member_field = jnp.dot(picked, basis, preferred_element_type=jnp.float32)  14.4 us
    dot_general x1, matrix products, on_device(): lax.dot_general(basis, weighted, (((1,), (1,)), ((), ())), preferred_elem...  13.7 us
    dot_general x1, matrix products, on_device(): jnp.einsum('imj,msjlc->ilsc', select.reshape(member_dev, mem_count, membe...  8.11 us
    all_to_all x1, starting transfers between devices, on_device(): lax.all_to_all(outgoing, 'mem', split_axis=0, concat_axis=0, tiled=True)  4.62 us
    dot_general x1, local copies, waits for them, and re-layouts, on_device(): member_field = jnp.dot(picked, basis, preferred_element_type=jnp.float32)  4.19 us
  transfers between devices with their start and end apart: 4, of which 3 were waited for; matrix products, arithmetic and copies ran while one was open for 18% of the time, Pallas kernels for 0%

commit v1 on v0

v1 whole, which is shorter than its diff:
```python
import functools
import jax
import jax.numpy as jnp
from jax import lax
from jax.experimental import pallas as pl
from jax.experimental.pallas import tpu as pltpu
from jax.sharding import PartitionSpec as P

MESH = pl.DeviceIdType.MESH
F32 = jnp.float32
BF16 = jnp.bfloat16
NT = (((1,), (1,)), ((), ()))


def flip(a, k, n):
    out, bit = 0, 1
    while bit < n:
        out = out + lax.rem(lax.div(a, bit) + (k // bit) % 2, 2) * bit
        bit *= 2
    return out


def kernel(
    zn, sn, levels,
    table, gain, root, root_t, alpha, gradient, anomalies, basis,
    inc_out, grad_out,
    anom, base, weighted, coef_all, mine, pair_out, pair_in, rs_out, rs_in,
    pick_all, grad_all, acc, inc_own, inc_stage, inc_in, inc_red,
    anom_sem, base_sem, z_send, z_recv, pair_send, pair_recv, rs_send, rs_recv,
    pk_send, pk_recv, fw_send, fw_recv, g_send, g_recv, is_send, is_recv, ia_send, ia_recv,
):
    z = lax.axis_index("mem")
    s = lax.axis_index("state")
    chip, core = lax.div(s, 2), lax.rem(s, 2)
    qn = sn // 2
    partner = chip * 2 + (1 - core)
    rows, cols = alpha.shape
    columns = anom.shape[1]
    members = rows // levels
    high = lax.Precision.HIGHEST

    zpeer = [flip(z, k, zn) for k in range(zn)]
    qpeer = [flip(chip, k, qn) for k in range(qn)]

    def load_of(t, n):
        return pltpu.make_async_copy(basis.at[t], base.at[t], base_sem.at[n])

    order_of_q = list(range(qn - 1, -1, -1))
    anom_copy = pltpu.make_async_copy(anomalies, anom, anom_sem)
    anom_copy.start()
    loads = []
    for i, k in enumerate(order_of_q):
        loads.append((load_of(qpeer[k] * 2 + 1 - core, 2 * i), load_of(qpeer[k] * 2 + core, 2 * i + 1)))
        loads[-1][0].start()
        loads[-1][1].start()

    barrier = pltpu.get_barrier_semaphore()
    for k in range(1, zn):
        pl.semaphore_signal(barrier, inc=1, device_id={"mem": zpeer[k]}, device_id_type=MESH)
    for k in range(1, qn):
        pl.semaphore_signal(barrier, inc=1, device_id={"state": qpeer[k] * 2 + core}, device_id_type=MESH)
    pl.semaphore_signal(barrier, inc=1, device_id={"state": partner}, device_id_type=MESH)

    def to(src, dst, send, recv, **where):
        return pltpu.make_async_remote_copy(
            src_ref=src, dst_ref=dst, send_sem=send, recv_sem=recv, device_id=where, device_id_type=MESH
        )

    own_rows = pl.ds(z * members, members)
    coef = jnp.dot(root[...], alpha[...].astype(F32), precision=high, preferred_element_type=F32)
    coef_all[own_rows] = (coef * gain[...]).astype(BF16).reshape(members, levels, -1)
    pl.semaphore_wait(barrier, zn - 1 + qn)
    z_copies = [
        to(coef_all.at[own_rows], coef_all.at[own_rows], z_send.at[k], z_recv.at[k], mem=zpeer[k])
        for k in range(1, zn)
    ]
    for copy in z_copies:
        copy.start()

    anom_copy.wait()

    def weigh(m, carry):
        at = pl.ds(pl.multiple_of(m * levels, levels), levels)
        weighted[at, :] = (anom[at, :].astype(F32) * gradient[...].astype(F32)).astype(BF16)
        return carry

    lax.fori_loop(0, members, weigh, 0)

    pairs = [
        to(pair_out.at[i], pair_in.at[i], pair_send.at[i], pair_recv.at[i], state=partner) for i in range(qn)
    ]
    scatters = [
        to(rs_out.at[i], rs_in.at[i], rs_send.at[i], rs_recv.at[i], state=qpeer[k] * 2 + core)
        for i, k in enumerate(order_of_q[:-1])
    ]

    half = rows // 2

    def project(t, store):
        def part(h, carry):
            at = pl.ds(pl.multiple_of(h * half, half), half)
            store(at, lax.dot_general(weighted[at, :], base[t], NT, preferred_element_type=F32))
            return carry

        lax.fori_loop(0, 2, part, 0)

    def combine(i):
        pairs[i].wait_recv()
        total = mine[i] + pair_in[i]
        if i < qn - 1:
            rs_out[i] = total.astype(BF16)
            scatters[i].start()
        else:
            mine[i] = total

    for i, k in enumerate(order_of_q):
        loads[i][0].wait()

        def put_pair(at, v, i=i):
            pair_out[i, at, :] = v

        def put_mine(at, v, i=i):
            mine[i, at, :] = v

        project(qpeer[k] * 2 + 1 - core, put_pair)
        pairs[i].start()
        if i > 0:
            combine(i - 1)
        loads[i][1].wait()
        project(qpeer[k] * 2 + core, put_mine)

    for copy in z_copies:
        copy.wait_recv()
    for m in range(members):
        pick_all[s, pl.ds(m * levels, levels), :] = coef_all[table[0, m]]
    picks = [to(pick_all.at[s], pick_all.at[s], pk_send.at[0], pk_recv.at[0], state=partner)] + [
        to(pick_all.at[s], pick_all.at[s], pk_send.at[k], pk_recv.at[k], state=qpeer[k] * 2 + core)
        for k in range(1, qn)
    ]
    for copy in picks:
        copy.start()
    combine(qn - 1)

    pieces = zn
    width = columns // pieces

    def spread(t, first):
        def part(j, carry):
            at = pl.ds(pl.multiple_of(j * width, width), width)
            field = jnp.dot(pick_all[t], base[t, :, at], preferred_element_type=F32)
            acc[:, at] = field if first else acc[:, at] + field
            return carry

        lax.fori_loop(0, pieces, part, 0)

    spread(s, True)
    picks[0].wait_recv()
    spread(partner, False)

    for copy in scatters:
        copy.wait_recv()
    total = mine[qn - 1]
    for i in range(qn - 1):
        total = total + rs_in[i].astype(F32)
    grad = jnp.dot(root_t[...], total, precision=high, preferred_element_type=F32)
    grad_all[own_rows] = (grad * gain[...]).astype(BF16).reshape(members, levels, -1)
    g_copies = [
        to(grad_all.at[own_rows], grad_all.at[own_rows], g_send.at[k], g_recv.at[k], mem=zpeer[k])
        for k in range(1, zn)
    ]
    for copy in g_copies:
        copy.start()

    forwards = [None]
    for k in range(1, qn):
        t, o = qpeer[k] * 2 + core, qpeer[k] * 2 + 1 - core
        picks[k].wait_recv()
        forwards.append(to(pick_all.at[t], pick_all.at[t], fw_send.at[k], fw_recv.at[k], state=partner))
        forwards[k].start()
        spread(t, False)
        forwards[k].wait_recv()
        if k < qn - 1:
            spread(o, False)

    last = qpeer[qn - 1] * 2 + 1 - core
    sums = [None] + [
        to(inc_stage.at[k], inc_in.at[k], is_send.at[k], is_recv.at[k], mem=zpeer[k]) for k in range(1, zn)
    ]
    for k in list(range(1, zn)) + [0]:
        at = pl.ds(pl.multiple_of(zpeer[k] * width, width), width)

        def one(m, run, at=at):
            here = pl.ds(pl.multiple_of(m * 4 * levels, 4 * levels), 4 * levels)
            field = acc[here, at] + jnp.dot(pick_all[last, here, :], base[last, :, at], preferred_element_type=F32)
            prod = field * anom[here, at].astype(F32)
            for u in range(4):
                run = run + prod[u * levels : (u + 1) * levels]
            return run

        run = jnp.zeros((levels, width), F32)
        for m in range(members // 4):
            run = one(m, run)
        if k > 0:
            inc_stage[k] = run.astype(BF16)
            sums[k].start()
        else:
            inc_own[...] = run
    run = inc_own[...]
    for k in range(1, zn):
        sums[k].wait_recv()
        run = run + inc_in[k].astype(F32)
    inc_red[z] = run.astype(BF16)
    shares = [
        to(inc_red.at[z], inc_red.at[z], ia_send.at[k], ia_recv.at[k], mem=zpeer[k]) for k in range(1, zn)
    ]
    for copy in shares:
        copy.start()

    for copy in g_copies:
        copy.wait_recv()
    for m in range(members):
        grad_out[pl.ds(m * levels, levels), :] = grad_all[table[1, m]].astype(F32)

    for copy in shares:
        copy.wait_recv()
    for b in range(zn):
        inc_out[:, b * width : (b + 1) * width] = inc_red[b].astype(F32)
    for copy in z_copies + pairs + scatters + picks + forwards[1:] + g_copies + sums[1:] + shares:
        copy.wait_send()


def on_device(zn, sn, anomalies, alpha, basis, gradient, vertical_root, band_gain, band, order):
    z = lax.axis_index("mem")
    members, levels, columns = anomalies.shape
    mode_rows = alpha.shape[2]
    bands = band_gain.shape[0]
    rows = members * levels
    onehot = (band[:, None] == jnp.arange(bands, dtype=jnp.int32)[None, :]).astype(F32)
    gain = jnp.sum(onehot * band_gain[None, :], axis=1)[None, :]
    block = jnp.arange(rows, dtype=jnp.int32) // levels
    same = block[:, None] == block[None, :]
    root = jnp.where(same, jnp.tile(vertical_root, (members, members)), 0.0)
    root_t = jnp.where(same, jnp.tile(vertical_root.T, (members, members)), 0.0)
    here = z * members + jnp.arange(members, dtype=jnp.int32)
    slots = jnp.arange(order.shape[0], dtype=jnp.int32)
    slot_of = jnp.sum(jnp.where(order[None, :] == here[:, None], slots[None, :], 0), axis=1)
    member_of = jnp.sum(jnp.where(slots[None, :] == here[:, None], order[None, :], 0), axis=1)
    table = jnp.stack([slot_of, member_of])
    qn = sn // 2
    width = columns // zn
    vmem = pl.BlockSpec(memory_space=pltpu.VMEM)
    hbm = pl.BlockSpec(memory_space=pl.ANY)
    dma = pltpu.SemaphoreType.DMA
    increment, grads = pl.pallas_call(
        functools.partial(kernel, zn, sn, levels),
        out_shape=(
            jax.ShapeDtypeStruct((levels, columns), F32),
            jax.ShapeDtypeStruct((rows, mode_rows), F32),
        ),
        in_specs=[pl.BlockSpec(memory_space=pltpu.SMEM)] + [vmem] * 5 + [hbm] * 2,
        out_specs=(vmem, vmem),
        scratch_shapes=[
            pltpu.VMEM((rows, columns), BF16),
            pltpu.VMEM((sn, mode_rows, columns), BF16),
            pltpu.VMEM((rows, columns), BF16),
            pltpu.VMEM((zn * members, levels, mode_rows), BF16),
            pltpu.VMEM((qn, rows, mode_rows), F32),
            pltpu.VMEM((qn, rows, mode_rows), F32),
            pltpu.VMEM((qn, rows, mode_rows), F32),
            pltpu.VMEM((qn, rows, mode_rows), BF16),
            pltpu.VMEM((qn, rows, mode_rows), BF16),
            pltpu.VMEM((sn, rows, mode_rows), BF16),
            pltpu.VMEM((zn * members, levels, mode_rows), BF16),
            pltpu.VMEM((rows, columns), F32),
            pltpu.VMEM((levels, width), F32),
            pltpu.VMEM((zn, levels, width), BF16),
            pltpu.VMEM((zn, levels, width), BF16),
            pltpu.VMEM((zn, levels, width), BF16),
            dma, dma((sn,)), dma((zn,)), dma((zn,)), dma((qn,)), dma((qn,)), dma((qn,)), dma((qn,)),
            dma((qn,)), dma((qn,)), dma((qn,)), dma((qn,)), dma((zn,)), dma((zn,)), dma((zn,)), dma((zn,)),
            dma((zn,)), dma((zn,)),
        ],
        compiler_params=pltpu.CompilerParams(
            collective_id=0, has_side_effects=True, vmem_limit_bytes=58 * 2**20
        ),
    )(
        table, gain, root, root_t, alpha.reshape(rows, mode_rows), gradient,
        anomalies.reshape(rows, columns), basis.reshape(sn, mode_rows, columns),
    )
    return increment, grads.reshape(members, levels, mode_rows)


def solution(mesh):
    zn, sn = mesh.shape["mem"], mesh.shape["state"]
    return jax.shard_map(
        functools.partial(on_device, zn, sn),
        mesh=mesh,
        in_specs=(
            P("mem", None, "state"),
            P("mem", None, "state"),
            P(None, "state"),
            P(None, "state"),
            P(),
            P(),
            P("state"),
            P(),
        ),
        out_specs=(P(None, "state"), P("mem", None, "state")),
        check_vma=False,
    )
```

time: 207 us -> 93.9 us (0.45)
  waiting for transfers between devices: 129 us -> 0 us
  Pallas kernels: 0 us -> 72.8 us
  matrix products: 40.2 us -> 0 us
  between operations: 15.6 us -> 0.69 us
  starting transfers between devices: 4.71 us -> 0 us
  local copies, waits for them, and re-layouts: 11.9 us -> 16.3 us
    pallas_call x0 -> x1, Pallas kernels: none -> 72.8 us  [on_device(): pl.pallas_call(functools.partial(kernel, zn, sn, levels), out_shape=(jax....]
    reduce_scatter x1 -> x0, waiting for transfers between devices: 52.4 us -> none  [on_device(): lax.psum_scatter(lax.dot_general(basis, weighted, (((1,), (1,)), ((), ())...]
    all_gather x1 -> x0, waiting for transfers between devices: 41 us -> none  [on_device(): gathered = lax.all_gather(coef[None], ('mem', 'state'), axis=0, tiled=True)]
    dot_general x6 -> x0, matrix products: 40.2 us -> none  [the longest x1 14.4 us: on_device(): member_field = jnp.dot(picked, basis, preferred_element_type=jnp.float32)]
    psum x1 -> x0, waiting for transfers between devices: 36.1 us -> none  [on_device(): increment = lax.psum(partial_value, 'mem')]
    another operation x0 -> x4, local copies, waits for them, and re-layouts: none -> 11.8 us  [the longest x2 5.9 us: on_device(): root = jnp.where(same, jnp.tile(vertical_root, (members, members)), 0.0)]
    all_to_all x1 -> x0, starting transfers between devices: 4.62 us -> none  [on_device(): lax.all_to_all(outgoing, 'mem', split_axis=0, concat_axis=0, tiled=True)]
    convert_element_type x2 -> x0, other arithmetic: 4.35 us -> none  [the longest x1 3.33 us: on_device(): (anomalies.astype(jnp.float32) * gradient.astype(jnp.float32)[None]).asty...]
  transfers between devices with their start and end apart: 4 -> 0, of which waited for: 3 -> 0; matrix products, arithmetic and copies ran while one was open for 18% -> 0% of each run, Pallas kernels for 0% -> 0%
where the time goes in v1:
time: 93.9 us; the launch traced here: 93.5 us
  Pallas kernels  72.8 us (78%)
  local copies, waits for them, and re-layouts  16.3 us (17%)
  other arithmetic  3.63 us (4%)
    pallas_call x1, Pallas kernels, on_device(): pl.pallas_call(functools.partial(kernel, zn, sn, levels), out_shape=(jax....  72.8 us
    another operation x2, local copies, waits for them, and re-layouts, on_device(): root = jnp.where(same, jnp.tile(vertical_root, (members, members)), 0.0)  5.9 us
    another operation x2, local copies, waits for them, and re-layouts, on_device(): root_t = jnp.where(same, jnp.tile(vertical_root.T, (members, members)), 0.0)  5.88 us
    unnamed x8, local copies, waits for them, and re-layouts  3.76 us

profile of v1, /device:TPU:0, one launch (start us, length us, event | category | flops | bytes accessed | tf_op | source)
XLA Modules:
  0.0 93.5 jit_solution(14566183127156178246)
XLA Ops:
  0.6 0.8 select_reduce_fusion.2
  1.5 0.6 pad_add_fusion.table
  2.1 0.8 copy.11
  2.8 0.0 copy-start
  2.8 2.3 %tile.20 = f32[16,32,16,32]{3,2,1,0:T(8,128)} broadcast(f32[32,32]{1,0:T(8,128)S(1)} %copy.11), dimensions={1,3} | broadcast | bytes 1052672 | tf_op jit(solution)/shard_map/tile | solution.py:243
  5.2 3.5 %tile.21 = f32[512,512]{1,0:T(8,128)S(1)} reshape(f32[16,32,16,32]{3,2,1,0:T(8,128)} %tile.20) | data formatting | bytes 2097152 | tf_op jit(solution)/shard_map/tile | solution.py:243
  8.7 0.0 copy-done
  8.7 2.3 %tile.8 = f32[16,32,16,32]{3,2,1,0:T(8,128)} broadcast(f32[32,32]{1,0:T(8,128)S(1)} %copy-done), dimensions={1,3} | broadcast | bytes 1052672 | tf_op jit(solution)/shard_map/tile | solution.py:242
  11.1 0.0 copy-start.1
  11.1 0.0 copy-start.2
  11.1 3.6 %tile.9 = f32[512,512]{1,0:T(8,128)S(1)} reshape(f32[16,32,16,32]{3,2,1,0:T(8,128)} %tile.8) | data formatting | bytes 2097152 | tf_op jit(solution)/shard_map/tile | solution.py:242
  14.7 1.6 %compare_select_fusion = (f32[512,512]{1,0:T(8,128)}, f32[512,512]{1,0:T(8,128)}) fusion(f32[512,512]{1,0:T(8,128)S(1)} %tile.21, s32[512]{0:T(512)S(1)} %add_select_fusion, f32[512,512]{1,0:T(8,128)S(1)} %tile.9), kind=kLoop, calls=%fused_computation | loop fusion | flops 786432 | bytes 4196352 | tf_op jit(solution)/shard_map/jit(_where)/select_n | solution.py:243
  16.2 0.0 copy-done.1
  16.2 0.0 copy-done.2
  16.2 0.6 select_reduce_fusion
  16.9 72.8 %shard_map.95 = (f32[32,4096]{1,0:T(8,128)}, f32[512,256]{1,0:T(8,128)}) custom-call(s32[2,16]{1,0:T(2,128)} %pad_add_fusion.table, f32[1,256]{1,0:T(1,128)} %bitcast.17, f32[512,512]{1,0:T(8,128)} %get-tuple-element.9.root, f32[512,512]{1,0:T(8,128)} %get-tuple-element.8.root_t, bf16[512,256]{1,0:T(8,128)(2,1)} %bitcast.15, bf16[32,4096]{1,0:T(8,128)(2,1)} %gradient.1, ...), custom_call_target="tpu_custom_call" | custom-call | tf_op jit(solution)/shard_map/pallas_call | solution.py:254
  89.7 1.9 %copy.14 = f32[32,4096]{1,0:T(8,128)} copy(f32[32,4096]{1,0:T(8,128)} %get-tuple-element.12) | data formatting | bytes 1048576
  91.6 1.9 %copy.15 = f32[16,32,256]{2,1,0:T(8,128)} copy(f32[16,32,256]{2,1,0:T(8,128)} %bitcast.14) | data formatting | bytes 1048576
  (2 shorter events, 0.0 us)
Async XLA Ops:
  2.8 5.9 %copy-start = (f32[32,32]{1,0:T(8,128)S(1)}, f32[32,32]{1,0:T(8,128)}, u32[]{:S(2)}) copy-start(f32[32,32]{1,0:T(8,128)} %param.12) | copy-start | bytes 12292
  11.1 5.2 %copy-start.1 = (s32[256]{0:T(256)S(1)}, s32[256]{0:T(256)}, u32[]{:S(2)}) copy-start(s32[256]{0:T(256)} %param.14) | copy-start | bytes 3076
  11.1 5.2 %copy-start.2 = (f32[16]{0:T(128)S(1)}, f32[16]{0:T(128)}, u32[]{:S(2)}) copy-start(f32[16]{0:T(128)} %param.13) | copy-start | bytes 196

commit v2 on v1

--- a/solution.py
+++ b/solution.py
@@ -22,10 +22,10 @@
 
 def kernel(
     zn, sn, levels,
-    table, gain, root, root_t, alpha, gradient, anomalies, basis,
+    table, gain, vroot, alpha, gradient, anomalies, basis,
     inc_out, grad_out,
     anom, base, weighted, coef_all, mine, pair_out, pair_in, rs_out, rs_in,
-    pick_all, grad_all, acc, inc_own, inc_stage, inc_in, inc_red,
+    pick_all, grad_all, acc, inc_own, inc_stage, inc_in, inc_red, pack, got,
     anom_sem, base_sem, z_send, z_recv, pair_send, pair_recv, rs_send, rs_recv,
     pk_send, pk_recv, fw_send, fw_recv, g_send, g_recv, is_send, is_recv, ia_send, ia_recv,
 ):
@@ -67,15 +67,96 @@
         )
 
     own_rows = pl.ds(z * members, members)
-    coef = jnp.dot(root[...], alpha[...].astype(F32), precision=high, preferred_element_type=F32)
+    line = zn == 4
+    outer = lax.div(lax.rem(z + 1, zn), 2) == 0
+    inner = jnp.logical_not(outer)
+
+    class Exchange:
+        def __init__(self, row, held, mine, packed, send, recv):
+            self.row, self.held, self.mine, self.packed = row, held, mine, packed
+            own = held.at[own_rows]
+            if not line:
+                self.copies = [
+                    to(own, own, send.at[k], recv.at[k], mem=zpeer[k]) for k in range(1, zn)
+                ]
+                return
+            self.near = 1 + lax.rem(z, 2)
+            self.far = lax.max(z - 1, 0) * 3 - lax.max(z - 2, 0) * 3
+            rim = held.at[pl.ds(self.far * members, members)]
+            kind = lax.rem(lax.div(z + 1, 2), 2)
+            self.first = to(own, own, send.at[0], recv.at[kind], mem=self.near)
+            self.from_rim = to(own, own, send.at[0], recv.at[0], mem=self.near)
+            self.from_inner = to(own, own, send.at[0], recv.at[1], mem=self.near)
+            self.relay = to(rim, rim, send.at[1], recv.at[2], mem=self.near)
+            self.give = to(packed, mine, send.at[2], recv.at[3], mem=self.far)
+
+        def start(self):
+            for copy in [self.first] if line else self.copies:
+                copy.start()
+
+        def pass_on(self):
+            if line:
+
+                @pl.when(inner)
+                def _():
+                    self.from_rim.wait_recv()
+                    self.relay.start()
+
+        def pick(self, out, who):
+            for m in range(members):
+                out[pl.ds(m * levels, levels), :] = self.held[table[self.row, who * members + m]]
+
+        def finish(self):
+            if not line:
+                for copy in self.copies:
+                    copy.wait_recv()
+                self.pick(self.mine, z)
+                return
+
+            @pl.when(inner)
+            def _():
+                self.from_inner.wait_recv()
+                self.relay.wait_recv()
+                self.pick(self.packed, self.far)
+                self.give.start()
+                self.pick(self.mine, z)
+
+        def settle(self):
+            if line:
+
+                @pl.when(outer)
+                def _():
+                    self.give.wait_recv()
+
+        def drain(self):
+            if not line:
+                for copy in self.copies:
+                    copy.wait_send()
+                return
+            self.first.wait_send()
+
+            @pl.when(inner)
+            def _():
+                self.relay.wait_send()
+                self.give.wait_send()
+
+    row_of = lax.broadcasted_iota(jnp.int32, (rows, levels), 0)
+    level_of = lax.broadcasted_iota(jnp.int32, (rows, levels), 1)
+    expand = jnp.where(lax.rem(row_of, levels) == level_of, 1.0, 0.0).astype(F32)
+    here_of = lax.broadcasted_iota(jnp.int32, (rows, rows), 0)
+    there_of = lax.broadcasted_iota(jnp.int32, (rows, rows), 1)
+    same = lax.div(here_of, levels) == lax.div(there_of, levels)
+
+    def blocks(tall):
+        full = lax.dot_general(tall, expand, NT, precision=high, preferred_element_type=F32)
+        return jnp.where(same, full, 0.0)
+
+    root = blocks(jnp.dot(expand, vroot[...], precision=high, preferred_element_type=F32))
+    coef = jnp.dot(root, alpha[...].astype(F32), precision=high, preferred_element_type=F32)
     coef_all[own_rows] = (coef * gain[...]).astype(BF16).reshape(members, levels, -1)
     pl.semaphore_wait(barrier, zn - 1 + qn)
-    z_copies = [
-        to(coef_all.at[own_rows], coef_all.at[own_rows], z_send.at[k], z_recv.at[k], mem=zpeer[k])
-        for k in range(1, zn)
-    ]
-    for copy in z_copies:
-        copy.start()
+    coef_ex = Exchange(0, coef_all, pick_all.at[s], pack.at[0], z_send, z_recv)
+    coef_ex.start()
 
     anom_copy.wait()
 
@@ -128,18 +209,18 @@
             combine(i - 1)
         loads[i][1].wait()
         project(qpeer[k] * 2 + core, put_mine)
-
-    for copy in z_copies:
-        copy.wait_recv()
-    for m in range(members):
-        pick_all[s, pl.ds(m * levels, levels), :] = coef_all[table[0, m]]
+        if i == qn // 2 - 1:
+            coef_ex.pass_on()
+
+    coef_ex.finish()
+    combine(qn - 1)
+    coef_ex.settle()
     picks = [to(pick_all.at[s], pick_all.at[s], pk_send.at[0], pk_recv.at[0], state=partner)] + [
         to(pick_all.at[s], pick_all.at[s], pk_send.at[k], pk_recv.at[k], state=qpeer[k] * 2 + core)
         for k in range(1, qn)
     ]
     for copy in picks:
         copy.start()
-    combine(qn - 1)
 
     pieces = zn
     width = columns // pieces
@@ -154,22 +235,18 @@
         lax.fori_loop(0, pieces, part, 0)
 
     spread(s, True)
-    picks[0].wait_recv()
-    spread(partner, False)
-
     for copy in scatters:
         copy.wait_recv()
     total = mine[qn - 1]
     for i in range(qn - 1):
         total = total + rs_in[i].astype(F32)
-    grad = jnp.dot(root_t[...], total, precision=high, preferred_element_type=F32)
+    root_t = blocks(lax.dot_general(expand, vroot[...], NT, precision=high, preferred_element_type=F32))
+    grad = jnp.dot(root_t, total, precision=high, preferred_element_type=F32)
     grad_all[own_rows] = (grad * gain[...]).astype(BF16).reshape(members, levels, -1)
-    g_copies = [
-        to(grad_all.at[own_rows], grad_all.at[own_rows], g_send.at[k], g_recv.at[k], mem=zpeer[k])
-        for k in range(1, zn)
-    ]
-    for copy in g_copies:
-        copy.start()
+    grad_ex = Exchange(1, grad_all, got, pack.at[1], g_send, g_recv)
+    grad_ex.start()
+    picks[0].wait_recv()
+    spread(partner, False)
 
     forwards = [None]
     for k in range(1, qn):
@@ -181,6 +258,8 @@
         forwards[k].wait_recv()
         if k < qn - 1:
             spread(o, False)
+        if k == qn // 2:
+            grad_ex.pass_on()
 
     last = qpeer[qn - 1] * 2 + 1 - core
     sums = [None] + [
@@ -205,6 +284,7 @@
             sums[k].start()
         else:
             inc_own[...] = run
+    grad_ex.finish()
     run = inc_own[...]
     for k in range(1, zn):
         sums[k].wait_recv()
@@ -216,36 +296,29 @@
     for copy in shares:
         copy.start()
 
-    for copy in g_copies:
-        copy.wait_recv()
-    for m in range(members):
-        grad_out[pl.ds(m * levels, levels), :] = grad_all[table[1, m]].astype(F32)
+    grad_ex.settle()
+    grad_out[...] = got[...]
 
     for copy in shares:
         copy.wait_recv()
     for b in range(zn):
-        inc_out[:, b * width : (b + 1) * width] = inc_red[b].astype(F32)
-    for copy in z_copies + pairs + scatters + picks + forwards[1:] + g_copies + sums[1:] + shares:
+        inc_out[:, b * width : (b + 1) * width] = inc_red[b]
+    coef_ex.drain()
+    grad_ex.drain()
+    for copy in pairs + scatters + picks + forwards[1:] + sums[1:] + shares:
         copy.wait_send()
 
 
 def on_device(zn, sn, anomalies, alpha, basis, gradient, vertical_root, band_gain, band, order):
-    z = lax.axis_index("mem")
     members, levels, columns = anomalies.shape
     mode_rows = alpha.shape[2]
     bands = band_gain.shape[0]
     rows = members * levels
     onehot = (band[:, None] == jnp.arange(bands, dtype=jnp.int32)[None, :]).astype(F32)
     gain = jnp.sum(onehot * band_gain[None, :], axis=1)[None, :]
-    block = jnp.arange(rows, dtype=jnp.int32) // levels
-    same = block[:, None] == block[None, :]
-    root = jnp.where(same, jnp.tile(vertical_root, (members, members)), 0.0)
-    root_t = jnp.where(same, jnp.tile(vertical_root.T, (members, members)), 0.0)
-    here = z * members + jnp.arange(members, dtype=jnp.int32)
     slots = jnp.arange(order.shape[0], dtype=jnp.int32)
-    slot_of = jnp.sum(jnp.where(order[None, :] == here[:, None], slots[None, :], 0), axis=1)
-    member_of = jnp.sum(jnp.where(slots[None, :] == here[:, None], order[None, :], 0), axis=1)
-    table = jnp.stack([slot_of, member_of])
+    slot_of = jnp.sum(jnp.where(order[None, :] == slots[:, None], slots[None, :], 0), axis=1)
+    table = jnp.stack([slot_of, order])
     qn = sn // 2
     width = columns // zn
     vmem = pl.BlockSpec(memory_space=pltpu.VMEM)
@@ -254,10 +327,10 @@
     increment, grads = pl.pallas_call(
         functools.partial(kernel, zn, sn, levels),
         out_shape=(
-            jax.ShapeDtypeStruct((levels, columns), F32),
-            jax.ShapeDtypeStruct((rows, mode_rows), F32),
+            jax.ShapeDtypeStruct((levels, columns), BF16),
+            jax.ShapeDtypeStruct((rows, mode_rows), BF16),
         ),
-        in_specs=[pl.BlockSpec(memory_space=pltpu.SMEM)] + [vmem] * 5 + [hbm] * 2,
+        in_specs=[pl.BlockSpec(memory_space=pltpu.SMEM)] + [vmem] * 4 + [hbm] * 2,
         out_specs=(vmem, vmem),
         scratch_shapes=[
             pltpu.VMEM((rows, columns), BF16),
@@ -276,6 +349,8 @@
             pltpu.VMEM((zn, levels, width), BF16),
             pltpu.VMEM((zn, levels, width), BF16),
             pltpu.VMEM((zn, levels, width), BF16),
+            pltpu.VMEM((2, rows, mode_rows), BF16),
+            pltpu.VMEM((rows, mode_rows), BF16),
             dma, dma((sn,)), dma((zn,)), dma((zn,)), dma((qn,)), dma((qn,)), dma((qn,)), dma((qn,)),
             dma((qn,)), dma((qn,)), dma((qn,)), dma((qn,)), dma((zn,)), dma((zn,)), dma((zn,)), dma((zn,)),
             dma((zn,)), dma((zn,)),
@@ -284,10 +359,10 @@
             collective_id=0, has_side_effects=True, vmem_limit_bytes=58 * 2**20
         ),
     )(
-        table, gain, root, root_t, alpha.reshape(rows, mode_rows), gradient,
+        table, gain, vertical_root, alpha.reshape(rows, mode_rows), gradient,
         anomalies.reshape(rows, columns), basis.reshape(sn, mode_rows, columns),
     )
-    return increment, grads.reshape(members, levels, mode_rows)
+    return increment.astype(F32), grads.astype(F32).reshape(members, levels, mode_rows)
 
 
 def solution(mesh):

time: 93.9 us -> 69.9 us (0.74)
  local copies, waits for them, and re-layouts: 16.3 us -> 0 us
  Pallas kernels: 72.8 us -> 62.2 us
  other arithmetic: 3.63 us -> 6.91 us
    another operation x4 -> x0, local copies, waits for them, and re-layouts: 11.8 us -> none  [the longest x2 5.9 us: on_device(): root = jnp.where(same, jnp.tile(vertical_root, (members, members)), 0.0)]
    pallas_call x1, Pallas kernels: 72.8 us -> 62.2 us  [on_device(): pl.pallas_call(functools.partial(kernel, zn, sn, levels), out_shape=(jax....]
    unnamed x8 -> x0, local copies, waits for them, and re-layouts: 3.76 us -> none
    reshape x0 -> x1, other arithmetic: none -> 1.79 us  [on_device(): grads.astype(F32).reshape(members, levels, mode_rows)]
    convert_element_type x0 -> x1, other arithmetic: none -> 1.78 us  [on_device(): increment.astype(F32)]
    select_n x2 -> x0, other arithmetic: 1.56 us -> none  [the longest x1 1.56 us: on_device(): root_t = jnp.where(same, jnp.tile(vertical_root.T, (members, members)), 0.0)]
where the time goes in v2:
time: 69.9 us; the launch traced here: 69.7 us
  Pallas kernels  62.2 us (89%)
  other arithmetic  6.91 us (10%)
    pallas_call x1, Pallas kernels, on_device(): pl.pallas_call(functools.partial(kernel, zn, sn, levels), out_shape=(jax....  62.2 us
    reshape x1, other arithmetic, on_device(): grads.astype(F32).reshape(members, levels, mode_rows)  1.79 us
    convert_element_type x1, other arithmetic, on_device(): increment.astype(F32)  1.78 us

profile of v2, /device:TPU:0, one launch (start us, length us, event | category | flops | bytes accessed | tf_op | source)
XLA Modules:
  0.0 69.7 jit_solution(1706499378336571084)
XLA Ops:
  0.6 0.8 %select_reduce_fusion = s32[64]{0:T(128)S(1)} fusion(s32[64]{0:T(128)} %param.15), kind=kLoop, calls=%fused_computation | loop fusion | flops 12224 | bytes 512 | tf_op jit(solution)/shard_map/reduce_sum | solution.py:320
  1.4 1.2 %pad_add_fusion.table = s32[2,64]{1,0:T(2,128)} fusion(s32[1,64]{1,0:T(1,128)} %bitcast.13, s32[1,64]{1,0:T(1,128)S(1)} %bitcast.14), kind=kLoop, calls=%fused_computation.4 | loop fusion | flops 128 | bytes 1024 | tf_op jit(solution)/shard_map/stack | solution.py:321
  2.6 1.3 %select_reduce_fusion.1 = f32[256]{0:T(256)} fusion(f32[16]{0:T(128)} %param.13, s32[256]{0:T(256)} %param.14), kind=kLoop, calls=%fused_computation.2 | loop fusion | flops 12032 | bytes 2112 | tf_op jit(solution)/shard_map/reduce_sum | solution.py:318
  4.0 62.2 %shard_map.95 = (bf16[32,4096]{1,0:T(8,128)(2,1)}, bf16[512,256]{1,0:T(8,128)(2,1)}) custom-call(s32[2,64]{1,0:T(2,128)} %pad_add_fusion.table, f32[1,256]{1,0:T(1,128)} %bitcast.12, f32[32,32]{1,0:T(8,128)} %vroot.1, bf16[512,256]{1,0:T(8,128)(2,1)} %bitcast.10, bf16[32,4096]{1,0:T(8,128)(2,1)} %gradient.1, bf16[512,4096]{1,0:T(8,128)(2,1)} %bitcast.9, ...), custom_call_target="tpu_custom_call" | custom-call | tf_op jit(solution)/shard_map/pallas_call | solution.py:327
  66.1 1.8 %convert.1 = f32[16,32,256]{2,1,0:T(8,128)} convert(bf16[16,32,256]{2,1,0:T(8,128)(2,1)} %bitcast.11) | non-fusion elementwise | flops 131072 | bytes 786432 | tf_op jit(solution)/shard_map/reshape | solution.py:365
  67.9 1.8 %convert_element_type.2 = f32[32,4096]{1,0:T(8,128)} convert(bf16[32,4096]{1,0:T(8,128)(2,1)} %get-tuple-element.4) | non-fusion elementwise | flops 131072 | bytes 786432 | tf_op jit(solution)/shard_map/convert_element_type | solution.py:365
